TPU v7x, 32 devices: a whole 2x2x4 slice. The times are simulated.
32 devices in a mesh: wide: 8 (over z, x), narrow: 4 (over y, core).
Axes of the slice: x: 2, y: 2, z: 4, core: 2. Of those that a mesh axis runs over, the one named last changes fastest.
Arguments:
- cost: float32 [1024, 16384], P('wide', 'narrow'), may hold values from 0 to 2
- plan: float32 [1024, 16384], P('wide', 'narrow'), may hold values from 0 to 2
- row_mass: float32 [1024], P('wide'), may hold values from 4096 to 28672
- col_mass: float32 [16384], P('narrow'), may hold values from 256 to 1792
- row_dual: float32 [1024], P('wide'), may hold values from -3 to 3
- col_dual: float32 [16384], P('narrow'), may hold values from -3 to 3
Outputs:
- plan_out: float32 [1024, 16384], P('wide', 'narrow')
- row_out: float32 [1024], P('wide')
- col_out: float32 [16384], P('narrow')
All inputs are finite; a program needn't handle non-finite values.
Results may differ from a plain program's by a relative error of at most 0.0001.
Values sent between devices are 32-bit elements; how exact they have to be, the bound alone decides.
A program may use at most 64 MiB of HBM per device.

v0:
```python
import math
import jax
import jax.numpy as jnp
from jax import lax
from jax.sharding import PartitionSpec as P

ITERS = 4


def shards(cost, plan, row_mass, col_mass, row_dual, col_dual):
    wide_count = lax.axis_size("wide")
    narrow_count = lax.axis_size("narrow")
    total_rows = plan.shape[0] * wide_count
    total_cols = plan.shape[1] * narrow_count
    step_base = 0.9 / math.sqrt(total_rows + total_cols)
    weight = jnp.float32(step_base)
    for step in range(ITERS):
        primal_step = step_base / weight
        dual_step = step_base * weight
        fresh = jnp.maximum(
            plan - primal_step * (cost - row_dual[:, None] - col_dual[None, :]), 0.0
        )
        change = fresh - plan
        extrap = fresh + change
        moved = jnp.sum(change * change)
        row_total = lax.psum(jnp.sum(extrap, axis=1), "narrow")
        new_row = row_dual + dual_step * (row_mass - row_total)
        row_square = jnp.sum((new_row - row_dual) ** 2)
        col_local = jnp.sum(extrap, axis=0)
        col_total = lax.psum(col_local, "wide")
        new_col = col_dual + dual_step * (col_mass - col_total)
        col_share = jnp.sum((new_col - col_dual) ** 2) / wide_count
        dual_share = row_square / narrow_count + col_share
        moved_all = lax.psum(moved, ("wide", "narrow"))
        dual_moved = lax.psum(dual_share, ("wide", "narrow"))
        weight = jnp.sqrt(weight * jnp.sqrt((dual_moved + 1.0) / (moved_all + 1.0)))
        plan, row_dual, col_dual = (fresh, new_row, new_col)
    return (plan, row_dual, col_dual)


def solution(mesh):
    in_specs = (
        P("wide", "narrow"),
        P("wide", "narrow"),
        P("wide"),
        P("narrow"),
        P("wide"),
        P("narrow"),
    )
    out_specs = (P("wide", "narrow"), P("wide"), P("narrow"))
    return jax.shard_map(shards, mesh=mesh, in_specs=in_specs, out_specs=out_specs, check_vma=False)
```

profile of v0, /device:TPU:0, one launch (start us, length us, event | category | flops | bytes accessed | tf_op | source)
XLA Modules:
  0.0 314.4 jit_solution(7714371782723744070)
XLA Ops:
  0.6 0.0 copy-start.1
  0.6 0.0 copy-start.3
  0.7 0.0 copy-start.2
  0.7 0.0 copy-start.4
  0.7 0.0 copy-start
  0.7 4.2 %multiply_reduce_fusion.2 = (f32[]{:T(128)}, f32[4096]{0:T(1024)S(1)}, f32[128]{0:T(128)S(1)}) fusion(f32[128,4096]{1,0:T(8,128)} %param.7, f32[4096]{0:T(1024)} %param.11, f32[128,4096]{1,0:T(8,128)} %param.6, f32[128]{0:T(128)} %param.10), kind=kLoop, calls=%fused_computation.6 | loop fusion | flops 5238655 | bytes 4228100 | tf_op jit(solution)/shard_map/reduce_sum | solution.py:25
  4.9 38.8 %psum.99 = f32[4096]{0:T(1024)S(1)} all-reduce(f32[4096]{0:T(1024)S(1)} %get-tuple-element.12), channel_id=1, replica_groups=mesh['wide'=8,'narrow'=4] {'wide'}, use_global_device_ids=true, to_apply=%region_4.0 | all-reduce | flops 4096 | bytes 32768 | tf_op jit(solution)/shard_map/psum | solution.py:30
  43.7 5.6 %psum.98 = f32[128]{0:T(128)S(1)} all-reduce(f32[128]{0:T(128)S(1)} %get-tuple-element.13), channel_id=1, replica_groups=mesh['wide'=8,'narrow'=4] {'narrow'}, use_global_device_ids=true, to_apply=%region_1.0 | all-reduce | flops 128 | bytes 1024 | tf_op jit(solution)/shard_map/psum | solution.py:26
  49.3 0.0 copy-done.3
  49.3 0.0 copy-done.4
  49.3 0.6 multiply_reduce_fusion.8
  50.6 0.0 copy-done.1
  50.6 0.0 copy-done.2
  50.6 0.6 multiply_reduce_fusion.5
  51.9 37.2 %all-reduce.2 = (f32[]{:T(128)}, f32[]{:T(128)}) all-reduce(f32[]{:T(128)S(6)} %add.94, f32[]{:T(128)} %get-tuple-element.11), channel_id=1, replica_groups=mesh['wide'=8,'narrow'=4] {'wide','narrow'}, use_global_device_ids=true, to_apply=%region_6.0 | all-reduce | flops 2 | bytes 16 | tf_op jit(solution)/shard_map/psum | solution.py:35
  90.5 0.0 copy-done
  90.5 3.7 %multiply_reduce_fusion.1 = (f32[]{:T(128)}, f32[128]{0:T(128)S(1)}, f32[4096]{0:T(1024)S(1)}) fusion(f32[4096]{0:T(1024)S(1)} %get-tuple-element.30, f32[128,4096]{1,0:T(8,128)} %param.6, f32[128]{0:T(128)S(1)} %get-tuple-element.32, f32[]{:T(128)S(6)} %div.39, f32[128,4096]{1,0:T(8,128)S(1)} %copy-done, f32[4096]{0:T(1024)S(1)} %copy-done.1, ...), kind=kLoop, calls=%fused_computation.4 | loop fusion | flops 7860095 | bytes 4245000 | tf_op jit(solution)/shard_map/reduce_sum | solution.py:25
  94.2 6.9 %psum.102 = f32[128]{0:T(128)S(1)} all-reduce(f32[128]{0:T(128)S(1)} %get-tuple-element.9), channel_id=1, replica_groups=mesh['wide'=8,'narrow'=4] {'narrow'}, use_global_device_ids=true, to_apply=%region_10.0 | all-reduce | flops 128 | bytes 1024 | tf_op jit(solution)/shard_map/psum | solution.py:26
  101.1 0.6 multiply_reduce_fusion.7
  102.4 35.6 %psum.103 = f32[4096]{0:T(1024)S(1)} all-reduce(f32[4096]{0:T(1024)S(1)} %get-tuple-element.10), channel_id=1, replica_groups=mesh['wide'=8,'narrow'=4] {'wide'}, use_global_device_ids=true, to_apply=%region_13.0 | all-reduce | flops 4096 | bytes 32768 | tf_op jit(solution)/shard_map/psum | solution.py:30
  138.0 0.6 multiply_reduce_fusion.4
  139.2 37.1 %all-reduce.1 = (f32[]{:T(128)}, f32[]{:T(128)}) all-reduce(f32[]{:T(128)S(6)} %add.100, f32[]{:T(128)} %get-tuple-element.8), channel_id=1, replica_groups=mesh['wide'=8,'narrow'=4] {'wide','narrow'}, use_global_device_ids=true, to_apply=%region_15.0 | all-reduce | flops 2 | bytes 16 | tf_op jit(solution)/shard_map/psum | solution.py:35
  177.8 4.2 %multiply_reduce_fusion = (f32[]{:T(128)}, f32[128]{0:T(128)S(1)}, f32[4096]{0:T(1024)S(1)}) fusion(f32[4096]{0:T(1024)S(1)} %get-tuple-element.26, f32[128,4096]{1,0:T(8,128)} %param.6, f32[128]{0:T(128)S(1)} %get-tuple-element.28, f32[]{:T(128)S(6)} %div.43, f32[4096]{0:T(1024)S(1)} %get-tuple-element.30, f32[128]{0:T(128)S(1)} %get-tuple-element.32, ...), kind=kLoop, calls=%fused_computation.2 | loop fusion | flops 10481535 | bytes 4261900 | tf_op jit(solution)/shard_map/reduce_sum | solution.py:25
  182.0 7.2 %psum.106 = f32[128]{0:T(128)S(1)} all-reduce(f32[128]{0:T(128)S(1)} %get-tuple-element.6), channel_id=1, replica_groups=mesh['wide'=8,'narrow'=4] {'narrow'}, use_global_device_ids=true, to_apply=%region_19.0 | all-reduce | flops 128 | bytes 1024 | tf_op jit(solution)/shard_map/psum | solution.py:26
  189.2 0.6 multiply_reduce_fusion.6
  190.5 35.3 %psum.107 = f32[4096]{0:T(1024)S(1)} all-reduce(f32[4096]{0:T(1024)S(1)} %get-tuple-element.7), channel_id=1, replica_groups=mesh['wide'=8,'narrow'=4] {'wide'}, use_global_device_ids=true, to_apply=%region_22.0 | all-reduce | flops 4096 | bytes 32768 | tf_op jit(solution)/shard_map/psum | solution.py:30
  225.8 0.6 multiply_reduce_fusion.3
  227.0 37.3 %all-reduce = (f32[]{:T(128)}, f32[]{:T(128)}) all-reduce(f32[]{:T(128)S(6)} %add.106, f32[]{:T(128)} %get-tuple-element.5), channel_id=1, replica_groups=mesh['wide'=8,'narrow'=4] {'wide','narrow'}, use_global_device_ids=true, to_apply=%region_24.0 | all-reduce | flops 2 | bytes 16 | tf_op jit(solution)/shard_map/psum | solution.py:35
  265.8 4.9 %fusion.6 = (f32[4096]{0:T(1024)S(1)}, f32[128]{0:T(128)S(1)}, f32[128,4096]{1,0:T(8,128)}) fusion(f32[4096]{0:T(1024)S(1)} %get-tuple-element.26, f32[128,4096]{1,0:T(8,128)} %param.6, f32[128]{0:T(128)S(1)} %get-tuple-element.28, f32[]{:T(128)S(6)} %div.43, f32[4096]{0:T(1024)S(1)} %get-tuple-element.30, f32[128]{0:T(128)S(1)} %get-tuple-element.32, ...), kind=kLoop, calls=%fused_computation.17 | loop fusion | flops 12054400 | bytes 6375948 | tf_op jit(solution)/shard_map/reduce_sum | solution.py:29
  270.7 36.8 %psum.111 = f32[4096]{0:T(1024)S(1)} all-reduce(f32[4096]{0:T(1024)S(1)} %get-tuple-element.3), channel_id=1, replica_groups=mesh['wide'=8,'narrow'=4] {'wide'}, use_global_device_ids=true, to_apply=%region_30.0 | all-reduce | flops 4096 | bytes 32768 | tf_op jit(solution)/shard_map/psum | solution.py:30
  307.5 0.6 multiply_add_fusion
  308.1 5.7 %psum.110 = f32[128]{0:T(128)S(1)} all-reduce(f32[128]{0:T(128)S(1)} %get-tuple-element.4), channel_id=1, replica_groups=mesh['wide'=8,'narrow'=4] {'narrow'}, use_global_device_ids=true, to_apply=%region_28.0 | all-reduce | flops 128 | bytes 1024 | tf_op jit(solution)/shard_map/psum | solution.py:26
  313.9 0.5 multiply_add_fusion.4
Async XLA Ops:
  0.6 49.9 %copy-start.1 = (f32[4096]{0:T(1024)S(1)}, f32[4096]{0:T(1024)}, u32[]{:S(2)}) copy-start(f32[4096]{0:T(1024)} %param.11) | copy-start | bytes 49156
  0.6 48.7 %copy-start.3 = (f32[128]{0:T(128)S(1)}, f32[128]{0:T(128)}, u32[]{:S(2)}) copy-start(f32[128]{0:T(128)} %param.10) | copy-start | bytes 1540
  0.7 49.9 %copy-start.2 = (f32[4096]{0:T(1024)S(1)}, f32[4096]{0:T(1024)}, u32[]{:S(2)}) copy-start(f32[4096]{0:T(1024)} %param.9) | copy-start | bytes 49156
  0.7 48.7 %copy-start.4 = (f32[128]{0:T(128)S(1)}, f32[128]{0:T(128)}, u32[]{:S(2)}) copy-start(f32[128]{0:T(128)} %param.8) | copy-start | bytes 1540
  0.7 89.8 %copy-start = (f32[128,4096]{1,0:T(8,128)S(1)}, f32[128,4096]{1,0:T(8,128)}, u32[]{:S(2)}) copy-start(f32[128,4096]{1,0:T(8,128)} %param.7) | copy-start | bytes 6291460
where the time goes:
time: 315 us; the launch traced here: 314 us
  blocking collectives  284 us (90%)
  other arithmetic  21.7 us (7%)
  between operations  9.03 us (3%)
    psum x4, blocking collectives, shards(): col_total = lax.psum(col_local, 'wide')  147 us
    psum x3, blocking collectives, shards(): dual_moved = lax.psum(dual_share, ('wide', 'narrow'))  112 us
    psum x4, blocking collectives, shards(): row_total = lax.psum(jnp.sum(extrap, axis=1), 'narrow')  25.5 us
    reduce_sum x3, other arithmetic, shards(): moved = jnp.sum(change * change)  12.1 us

commit v1 on v0

--- a/solution.py
+++ b/solution.py
@@ -32,7 +32,7 @@
         col_share = jnp.sum((new_col - col_dual) ** 2) / wide_count
         dual_share = row_square / narrow_count + col_share
         moved_all = lax.psum(moved, ("wide", "narrow"))
-        dual_moved = lax.psum(dual_share, ("wide", "narrow"))
+        dual_moved = lax.psum(lax.psum(dual_share, "narrow"), "wide")
         weight = jnp.sqrt(weight * jnp.sqrt((dual_moved + 1.0) / (moved_all + 1.0)))
         plan, row_dual, col_dual = (fresh, new_row, new_col)
     return (plan, row_dual, col_dual)

time: 315 us -> 390 us (1.24)
  blocking collectives: 284 us -> 358 us
    psum x3 -> x9, blocking collectives: 112 us -> 191 us  [the longest x3 118 us: shards(): moved_all = lax.psum(moved, ('wide', 'narrow'))]
where the time goes in v1:
time: 390 us; the launch traced here: 389 us
  blocking collectives  358 us (92%)
  other arithmetic  21.7 us (6%)
  between operations  9.06 us (2%)
    psum x4, blocking collectives, shards(): col_total = lax.psum(col_local, 'wide')  144 us
    psum x3, blocking collectives, shards(): moved_all = lax.psum(moved, ('wide', 'narrow'))  118 us
    psum x6, blocking collectives, shards(): dual_moved = lax.psum(lax.psum(dual_share, 'narrow'), 'wide')  72.2 us
    psum x4, blocking collectives, shards(): row_total = lax.psum(jnp.sum(extrap, axis=1), 'narrow')  23.6 us
    reduce_sum x3, other arithmetic, shards(): moved = jnp.sum(change * change)  12.1 us

profile of v1, /device:TPU:0, one launch (start us, length us, event | category | flops | bytes accessed | tf_op | source)
XLA Modules:
  0.0 389.3 jit_solution(6919098052084498544)
XLA Ops:
  0.6 0.0 copy-start.1
  0.6 0.0 copy-start.3
  0.7 0.0 copy-start.2
  0.7 0.0 copy-start.4
  0.7 0.0 copy-start
  0.7 4.2 %multiply_reduce_fusion.2 = (f32[]{:T(128)}, f32[4096]{0:T(1024)S(1)}, f32[128]{0:T(128)S(1)}) fusion(f32[128,4096]{1,0:T(8,128)} %param.7, f32[4096]{0:T(1024)} %param.11, f32[128,4096]{1,0:T(8,128)} %param.6, f32[128]{0:T(128)} %param.10), kind=kLoop, calls=%fused_computation.6 | loop fusion | flops 5238655 | bytes 4228100 | tf_op jit(solution)/shard_map/reduce_sum | solution.py:25
  4.9 42.2 %psum.123 = f32[]{:T(128)} all-reduce(f32[]{:T(128)} %get-tuple-element.11), channel_id=1, replica_groups=mesh['wide'=8,'narrow'=4] {'wide','narrow'}, use_global_device_ids=true, to_apply=%region_9.0 | all-reduce | flops 1 | bytes 8 | tf_op jit(solution)/shard_map/psum | solution.py:34
  47.7 36.8 %psum.120 = f32[4096]{0:T(1024)S(1)} all-reduce(f32[4096]{0:T(1024)S(1)} %get-tuple-element.12), channel_id=1, replica_groups=mesh['wide'=8,'narrow'=4] {'wide'}, use_global_device_ids=true, to_apply=%region_4.0 | all-reduce | flops 4096 | bytes 32768 | tf_op jit(solution)/shard_map/psum | solution.py:30
  84.4 5.6 %psum.119 = f32[128]{0:T(128)S(1)} all-reduce(f32[128]{0:T(128)S(1)} %get-tuple-element.13), channel_id=1, replica_groups=mesh['wide'=8,'narrow'=4] {'narrow'}, use_global_device_ids=true, to_apply=%region_1.0 | all-reduce | flops 128 | bytes 1024 | tf_op jit(solution)/shard_map/psum | solution.py:26
  90.0 0.0 copy-done.3
  90.0 0.0 copy-done.4
  90.0 0.6 multiply_reduce_fusion.8
  91.3 0.0 copy-done.1
  91.3 0.0 copy-done.2
  91.3 0.6 multiply_reduce_fusion.5
  92.6 6.7 %psum.121 = f32[]{:T(128)} all-reduce(f32[]{:T(128)S(6)} %add.100), channel_id=1, replica_groups=mesh['wide'=8,'narrow'=4] {'narrow'}, use_global_device_ids=true, to_apply=%region_6.0 | all-reduce | flops 1 | bytes 8 | tf_op jit(solution)/shard_map/psum | solution.py:35
  99.2 17.7 %psum.122 = f32[]{:T(128)} all-reduce(f32[]{:T(128)} %psum.121), channel_id=1, replica_groups=mesh['wide'=8,'narrow'=4] {'wide'}, use_global_device_ids=true, to_apply=%region_7.0 | all-reduce | flops 1 | bytes 8 | tf_op jit(solution)/shard_map/psum | solution.py:35
  117.8 0.0 copy-done
  117.8 3.7 multiply_reduce_fusion.1
  121.5 38.3 %psum.128 = f32[]{:T(128)} all-reduce(f32[]{:T(128)} %get-tuple-element.8), channel_id=1, replica_groups=mesh['wide'=8,'narrow'=4] {'wide','narrow'}, use_global_device_ids=true, to_apply=%region_19.0 | all-reduce | flops 1 | bytes 8 | tf_op jit(solution)/shard_map/psum | solution.py:34
  160.5 6.0 %psum.124 = f32[128]{0:T(128)S(1)} all-reduce(f32[128]{0:T(128)S(1)} %get-tuple-element.9), channel_id=1, replica_groups=mesh['wide'=8,'narrow'=4] {'narrow'}, use_global_device_ids=true, to_apply=%region_11.0 | all-reduce | flops 128 | bytes 1024 | tf_op jit(solution)/shard_map/psum | solution.py:26
  166.5 0.6 multiply_reduce_fusion.7
  167.8 36.4 %psum.125 = f32[4096]{0:T(1024)S(1)} all-reduce(f32[4096]{0:T(1024)S(1)} %get-tuple-element.10), channel_id=1, replica_groups=mesh['wide'=8,'narrow'=4] {'wide'}, use_global_device_ids=true, to_apply=%region_14.0 | all-reduce | flops 4096 | bytes 32768 | tf_op jit(solution)/shard_map/psum | solution.py:30
  204.2 0.6 multiply_reduce_fusion.4
  205.4 6.2 %psum.126 = f32[]{:T(128)} all-reduce(f32[]{:T(128)S(6)} %add.106), channel_id=1, replica_groups=mesh['wide'=8,'narrow'=4] {'narrow'}, use_global_device_ids=true, to_apply=%region_16.0 | all-reduce | flops 1 | bytes 8 | tf_op jit(solution)/shard_map/psum | solution.py:35
  211.6 17.7 %psum.127 = f32[]{:T(128)} all-reduce(f32[]{:T(128)} %psum.126), channel_id=1, replica_groups=mesh['wide'=8,'narrow'=4] {'wide'}, use_global_device_ids=true, to_apply=%region_17.0 | all-reduce | flops 1 | bytes 8 | tf_op jit(solution)/shard_map/psum | solution.py:35
  230.2 4.2 %multiply_reduce_fusion = (f32[]{:T(128)}, f32[128]{0:T(128)S(1)}, f32[4096]{0:T(1024)S(1)}) fusion(f32[4096]{0:T(1024)S(1)} %get-tuple-element.20, f32[128,4096]{1,0:T(8,128)} %param.6, f32[128]{0:T(128)S(1)} %get-tuple-element.22, f32[]{:T(128)S(6)} %div.43, f32[4096]{0:T(1024)S(1)} %get-tuple-element.24, f32[128]{0:T(128)S(1)} %get-tuple-element.26, ...), kind=kLoop, calls=%fused_computation.2 | loop fusion | flops 10481535 | bytes 4261900 | tf_op jit(solution)/shard_map/reduce_sum | solution.py:25
  234.4 38.0 %psum.133 = f32[]{:T(128)} all-reduce(f32[]{:T(128)} %get-tuple-element.5), channel_id=1, replica_groups=mesh['wide'=8,'narrow'=4] {'wide','narrow'}, use_global_device_ids=true, to_apply=%region_29.0 | all-reduce | flops 1 | bytes 8 | tf_op jit(solution)/shard_map/psum | solution.py:34
  273.0 6.4 %psum.129 = f32[128]{0:T(128)S(1)} all-reduce(f32[128]{0:T(128)S(1)} %get-tuple-element.6), channel_id=1, replica_groups=mesh['wide'=8,'narrow'=4] {'narrow'}, use_global_device_ids=true, to_apply=%region_21.0 | all-reduce | flops 128 | bytes 1024 | tf_op jit(solution)/shard_map/psum | solution.py:26
  279.4 0.6 multiply_reduce_fusion.6
  280.6 36.1 %psum.130 = f32[4096]{0:T(1024)S(1)} all-reduce(f32[4096]{0:T(1024)S(1)} %get-tuple-element.7), channel_id=1, replica_groups=mesh['wide'=8,'narrow'=4] {'wide'}, use_global_device_ids=true, to_apply=%region_24.0 | all-reduce | flops 4096 | bytes 32768 | tf_op jit(solution)/shard_map/psum | solution.py:30
  316.8 0.6 multiply_reduce_fusion.3
  318.0 6.2 %psum.131 = f32[]{:T(128)} all-reduce(f32[]{:T(128)S(6)} %add.112), channel_id=1, replica_groups=mesh['wide'=8,'narrow'=4] {'narrow'}, use_global_device_ids=true, to_apply=%region_26.0 | all-reduce | flops 1 | bytes 8 | tf_op jit(solution)/shard_map/psum | solution.py:35
  324.2 17.7 %psum.132 = f32[]{:T(128)} all-reduce(f32[]{:T(128)} %psum.131), channel_id=1, replica_groups=mesh['wide'=8,'narrow'=4] {'wide'}, use_global_device_ids=true, to_apply=%region_27.0 | all-reduce | flops 1 | bytes 8 | tf_op jit(solution)/shard_map/psum | solution.py:35
  342.8 4.9 %fusion.6 = (f32[4096]{0:T(1024)S(1)}, f32[128]{0:T(128)S(1)}, f32[128,4096]{1,0:T(8,128)}) fusion(f32[4096]{0:T(1024)S(1)} %get-tuple-element.20, f32[128,4096]{1,0:T(8,128)} %param.6, f32[128]{0:T(128)S(1)} %get-tuple-element.22, f32[]{:T(128)S(6)} %div.43, f32[4096]{0:T(1024)S(1)} %get-tuple-element.24, f32[128]{0:T(128)S(1)} %get-tuple-element.26, ...), kind=kLoop, calls=%fused_computation.17 | loop fusion | flops 12054400 | bytes 6375948 | tf_op jit(solution)/shard_map/reduce_sum | solution.py:29
  347.7 34.9 %psum.135 = f32[4096]{0:T(1024)S(1)} all-reduce(f32[4096]{0:T(1024)S(1)} %get-tuple-element.3), channel_id=1, replica_groups=mesh['wide'=8,'narrow'=4] {'wide'}, use_global_device_ids=true, to_apply=%region_33.0 | all-reduce | flops 4096 | bytes 32768 | tf_op jit(solution)/shard_map/psum | solution.py:30
  382.6 0.6 multiply_add_fusion
  383.2 5.6 %psum.134 = f32[128]{0:T(128)S(1)} all-reduce(f32[128]{0:T(128)S(1)} %get-tuple-element.4), channel_id=1, replica_groups=mesh['wide'=8,'narrow'=4] {'narrow'}, use_global_device_ids=true, to_apply=%region_31.0 | all-reduce | flops 128 | bytes 1024 | tf_op jit(solution)/shard_map/psum | solution.py:26
  388.8 0.5 multiply_add_fusion.4
Async XLA Ops:
  0.6 90.7 %copy-start.1 = (f32[4096]{0:T(1024)S(1)}, f32[4096]{0:T(1024)}, u32[]{:S(2)}) copy-start(f32[4096]{0:T(1024)} %param.11) | copy-start | bytes 49156
  0.6 89.4 %copy-start.3 = (f32[128]{0:T(128)S(1)}, f32[128]{0:T(128)}, u32[]{:S(2)}) copy-start(f32[128]{0:T(128)} %param.10) | copy-start | bytes 1540
  0.7 90.7 %copy-start.2 = (f32[4096]{0:T(1024)S(1)}, f32[4096]{0:T(1024)}, u32[]{:S(2)}) copy-start(f32[4096]{0:T(1024)} %param.9) | copy-start | bytes 49156
  0.7 89.4 %copy-start.4 = (f32[128]{0:T(128)S(1)}, f32[128]{0:T(128)}, u32[]{:S(2)}) copy-start(f32[128]{0:T(128)} %param.8) | copy-start | bytes 1540
  0.7 117.1 %copy-start = (f32[128,4096]{1,0:T(8,128)S(1)}, f32[128,4096]{1,0:T(8,128)}, u32[]{:S(2)}) copy-start(f32[128,4096]{1,0:T(8,128)} %param.7) | copy-start | bytes 6291460
